TPU v7x, 8 devices: a whole 2x2x1 slice. The times are simulated.
8 devices in a mesh: dp: 8 (over z, y, x, core).
Axes of the slice: x: 2, y: 2, z: 1, core: 2. Of those that a mesh axis runs over, the one named last changes fastest.
Arguments:
- x_in: bfloat16 [8192, 2048], P('dp')
- dy_mid: bfloat16 [8192, 5632], P('dp')
- x_mid: bfloat16 [8192, 5632], P('dp')
- dy_out: bfloat16 [8192, 2048], P('dp')
- w_fc1: float32 [2048, 5632], replicated
- w_fc2: float32 [5632, 2048], replicated
- stat_left: float32 [24, 1024, 1024], P('dp')
- stat_right: float32 [24, 1024, 1024], P('dp')
- root_left: float32 [24, 1024, 1024], P('dp')
- root_right: float32 [24, 1024, 1024], P('dp')
- graft_sq: float32 [24, 1024, 1024], P('dp')
- momentum: float32 [24, 1024, 1024], P('dp')
Outputs:
- output 1: float32 [2048, 5632], replicated
- output 2: float32 [5632, 2048], replicated
- output 3: float32 [24, 1024, 1024], P('dp')
- output 4: float32 [24, 1024, 1024], P('dp')
- output 5: float32 [24, 1024, 1024], P('dp')
- output 6: float32 [24, 1024, 1024], P('dp')
All inputs are finite; a program needn't handle non-finite values.
Results may differ from a plain program's by a relative error of at most 0.001.
Values are sent between devices in bfloat16 or wider.
A program may use at most 1.5 GiB of HBM per device.

v0:
```python
import jax
import jax.numpy as jnp
from jax import lax
from jax.sharding import PartitionSpec as P

STEP = 10
STAT_DECAY = 0.999
MOM_DECAY = 0.9
GRAFT_EPS = 1e-8
LEARN_RATE = 0.01
WEIGHT_DECAY = 1e-4
BIAS_CORR = 1.0 - STAT_DECAY ** STEP


def grad_blocks(x_rows, dy_rows, block_dim):
    n_tok, n_in = x_rows.shape
    n_out = dy_rows.shape[1]
    in_blocks = -(-n_in // block_dim)
    out_blocks = -(-n_out // block_dim)
    x_pad = jnp.pad(x_rows, ((0, 0), (0, in_blocks * block_dim - n_in))).reshape(n_tok, in_blocks, block_dim)
    dy_pad = jnp.pad(dy_rows, ((0, 0), (0, out_blocks * block_dim - n_out))).reshape(n_tok, out_blocks, block_dim)
    grad_tiles = jnp.einsum('tri,tcj->rcij', x_pad, dy_pad, preferred_element_type=jnp.float32)
    return grad_tiles.reshape(in_blocks * out_blocks, block_dim, block_dim)


def from_blocks(dir_blocks, n_rows, n_cols):
    block_dim = dir_blocks.shape[-1]
    row_blocks = -(-n_rows // block_dim)
    col_blocks = -(-n_cols // block_dim)
    full_mat = dir_blocks.reshape(row_blocks, col_blocks, block_dim, block_dim).transpose(0, 2, 1, 3)
    return full_mat.reshape(row_blocks * block_dim, col_blocks * block_dim)[:n_rows, :n_cols]


def keep_mask(block_ids, n_model, n_hidden, block_dim):
    model_blocks = -(-n_model // block_dim)
    hidden_blocks = -(-n_hidden // block_dim)
    half_count = model_blocks * hidden_blocks
    is_first = block_ids < half_count
    local_ids = block_ids % half_count
    row_first = jnp.minimum(n_model - (local_ids // hidden_blocks) * block_dim, block_dim)
    col_first = jnp.minimum(n_hidden - (local_ids % hidden_blocks) * block_dim, block_dim)
    row_second = jnp.minimum(n_hidden - (local_ids // model_blocks) * block_dim, block_dim)
    col_second = jnp.minimum(n_model - (local_ids % model_blocks) * block_dim, block_dim)
    row_count = jnp.where(is_first, row_first, row_second)
    col_count = jnp.where(is_first, col_first, col_second)
    offsets = jnp.arange(block_dim)
    return (offsets[None, :, None] < row_count[:, None, None]) & (offsets[None, None, :] < col_count[:, None, None])


def stat_update(grad_blk, stat_left, stat_right):
    left_prod = jnp.einsum('nik,njk->nij', grad_blk, grad_blk, precision=lax.Precision.HIGHEST, preferred_element_type=jnp.float32)
    right_prod = jnp.einsum('nki,nkj->nij', grad_blk, grad_blk, precision=lax.Precision.HIGHEST, preferred_element_type=jnp.float32)
    return STAT_DECAY * stat_left + (1.0 - STAT_DECAY) * left_prod, STAT_DECAY * stat_right + (1.0 - STAT_DECAY) * right_prod


def direction_update(grad_blk, root_left, root_right, graft_sq, momentum, keep_tiles):
    left_mul = jnp.einsum('nij,njk->nik', root_left, grad_blk, precision=lax.Precision.HIGHEST, preferred_element_type=jnp.float32)
    precond = jnp.einsum('nij,njk->nik', left_mul, root_right, precision=lax.Precision.HIGHEST, preferred_element_type=jnp.float32)
    precond = jnp.where(keep_tiles, precond, 0.0)
    new_sq = STAT_DECAY * graft_sq + (1.0 - STAT_DECAY) * grad_blk * grad_blk
    graft_dir = grad_blk / (jnp.sqrt(new_sq / BIAS_CORR) + GRAFT_EPS)
    graft_norm = jnp.sqrt(jnp.sum(graft_dir * graft_dir, axis=(1, 2)))
    pre_norm = jnp.sqrt(jnp.sum(precond * precond, axis=(1, 2)))
    new_mom = MOM_DECAY * momentum + precond * (graft_norm / pre_norm)[:, None, None]
    return new_sq, new_mom


def apply_update(w_fc1, w_fc2, dir_blocks):
    n_model, n_hidden = w_fc1.shape
    half_count = dir_blocks.shape[0] // 2
    dir_fc1 = from_blocks(dir_blocks[:half_count], n_model, n_hidden)
    dir_fc2 = from_blocks(dir_blocks[half_count:], n_hidden, n_model)
    new_w1 = w_fc1 - LEARN_RATE * (dir_fc1.astype(jnp.float32) + WEIGHT_DECAY * w_fc1)
    new_w2 = w_fc2 - LEARN_RATE * (dir_fc2.astype(jnp.float32) + WEIGHT_DECAY * w_fc2)
    return new_w1, new_w2


def solution(mesh):
    n_dev = mesh.shape['dp']

    def per_device(x_in, dy_mid, x_mid, dy_out, w_fc1, w_fc2, stat_left, stat_right, root_left, root_right, graft_sq, momentum):
        block_dim = stat_left.shape[-1]
        n_model, n_hidden = w_fc1.shape
        own_count = stat_left.shape[0]
        local_grad = jnp.concatenate([grad_blocks(x_in, dy_mid, block_dim), grad_blocks(x_mid, dy_out, block_dim)], axis=0)
        own_grad = lax.psum_scatter(local_grad, 'dp', scatter_dimension=0, tiled=True) / n_dev
        block_ids = lax.axis_index('dp') * own_count + jnp.arange(own_count)
        keep_tiles = keep_mask(block_ids, n_model, n_hidden, block_dim)
        new_left, new_right = stat_update(own_grad, stat_left, stat_right)
        new_sq, new_mom = direction_update(own_grad, root_left, root_right, graft_sq, momentum, keep_tiles)
        all_dir = lax.all_gather(new_mom.astype(jnp.bfloat16), 'dp', axis=0, tiled=True)
        new_w1, new_w2 = apply_update(w_fc1, w_fc2, all_dir)
        return new_w1, new_w2, new_left, new_right, new_sq, new_mom

    row_spec = P('dp', None)
    rep_spec = P(None, None)
    tile_spec = P('dp', None, None)
    in_specs = (row_spec, row_spec, row_spec, row_spec, rep_spec, rep_spec, tile_spec, tile_spec, tile_spec, tile_spec, tile_spec, tile_spec)
    out_specs = (rep_spec, rep_spec, tile_spec, tile_spec, tile_spec, tile_spec)
    return jax.shard_map(per_device, mesh=mesh, in_specs=in_specs, out_specs=out_specs, check_vma=False)
```

profile of v0, /device:TPU:0, one launch (start us, length us, event | category | flops | bytes accessed | tf_op | source)
XLA Modules:
  0.0 1422.8 jit_solution(4899917909870620222)
XLA Ops:
  7.2 0.0 reduce-scatter.2.cloned.1.call-start
  7.2 15.9 %copy.54 = bf16[1024,5632]{0,1:T(8,128)(2,1)} copy(bf16[1024,5632]{1,0:T(8,128)(2,1)} %param.13) | data formatting | bytes 23068672
  23.2 6.6 pad.7.clone
  29.8 33.3 %convolution_bitcast_fusion = f32[2,6,1024,1024]{2,3,0,1:T(8,128)} fusion(bf16[1024,6,1024,1]{0,2,3,1:T(8,128)(2,1)S(1)} %bitcast.59, bf16[128,2,8,1024]{3,2,1,0:T(8,128)(2,1)} %bitcast.60), kind=kOutput, calls=%fused_computation.3 | convolution fusion | flops 25769803776 | bytes 67108864 | tf_op jit(solution)/shard_map/tri,tcj->rcij/dot_general | solution.py:22
  63.1 49.5 %copy.38 = f32[2,6,1024,1024]{3,2,1,0:T(8,128)} copy(f32[2,6,1024,1024]{2,3,0,1:T(8,128)} %convolution_bitcast_fusion) | data formatting | bytes 100663296 | tf_op jit(solution)/shard_map/tri,tcj->rcij/transpose | solution.py:22
  112.6 15.9 %copy.55 = bf16[1024,5632]{0,1:T(8,128)(2,1)} copy(bf16[1024,5632]{1,0:T(8,128)(2,1)} %param.14) | data formatting | bytes 23068672
  128.5 6.6 pad.8.clone
  135.1 33.7 %fusion.9 = f32[6,1024,2,1024]{3,1,2,0:T(8,128)} fusion(bf16[1024,6,1024,1]{0,2,3,1:T(8,128)(2,1)S(1)} %bitcast.58, bf16[128,2,8,1024]{3,2,1,0:T(8,128)(2,1)} %bitcast.61), kind=kOutput, calls=%fused_computation.21 | convolution fusion | flops 25769803776 | bytes 67108864 | tf_op jit(solution)/shard_map/tri,tcj->rcij/dot_general | solution.py:22
  168.8 66.8 %pad_maximum_fusion = f32[24,1024,1024]{2,1,0:T(8,128)} fusion(f32[12,1024,1024]{2,1,0:T(8,128)} %bitcast.55, f32[12,1024,1024]{2,1,0:T(8,128)} %bitcast.48), kind=kLoop, calls=%fused_computation | loop fusion | flops 25165824 | bytes 201326592 | tf_op jit(solution)/shard_map/concatenate | solution.py:85
  235.7 0.0 reduce-scatter.2.cloned.1.call-update
  235.7 0.0 all-gather.2.cloned.1.call-start
  235.8 0.1 iota_compare_fusion
  235.8 0.1 iota_compare_fusion.1
  235.9 533.3 %reduce-scatter.2.cloned.1.call-done = f32[3,1024,1024]{2,1,0:T(8,128)} async-done(((f32[24,1024,1024]{2,1,0:T(8,128)}), f32[3,1024,1024]{2,1,0:T(8,128)}) %reduce-scatter.2.cloned.1.call-update) | async-done | bytes 12582928 | tf_op jit(solution)/shard_map/reduce_scatter | solution.py:86
  769.2 45.2 %fusion.4 = f32[3,1024,1024]{1,2,0:T(8,128)} fusion(f32[3,1024,1024]{2,1,0:T(8,128)} %param.20, f32[3,1024,1024]{2,1,0:T(8,128)} %reduce-scatter.2.cloned.1.call-done), kind=kOutput, calls=%fused_computation.15 | convolution fusion | flops 38657851392 | bytes 37748736 | tf_op jit(solution)/shard_map/nij,njk->nik/dot_general | solution.py:57
  814.4 48.6 %multiply_reduce_fusion = (f32[3]{0:T(128)S(1)}, f32[3,1024,1024]{2,1,0:T(8,128)}) fusion(pred[3,1024]{1,0:T(4,128)(4,1)S(1)} %iota_compare_fusion, pred[3,1024]{1,0:T(4,128)(4,1)S(1)} %iota_compare_fusion.1, f32[3,1024,1024]{1,2,0:T(8,128)} %fusion.4, f32[3,1024,1024]{2,1,0:T(8,128)} %param.21), kind=kOutput, calls=%fused_computation.7 | convolution fusion | flops 38667288576 | bytes 37754892 | tf_op jit(solution)/shard_map/nij,njk->nik/dot_general | solution.py:58
  863.0 0.0 slice-done.2
  863.1 13.6 multiply_reduce_fusion.1
  876.7 16.4 %fusion.25 = (bf16[3,1024,1024]{2,1,0:T(8,128)(2,1)}, f32[3,1024,1024]{2,1,0:T(8,128)}) fusion(f32[3]{0:T(128)S(1)} %rsqrt_multiply_fusion, f32[3,1024,1024]{2,1,0:T(8,128)} %get-tuple-element.25, pred[3,1024]{1,0:T(4,128)(4,1)S(1)} %iota_compare_fusion, pred[3,1024]{1,0:T(4,128)(4,1)S(1)} %iota_compare_fusion.1, f32[3,1024,1024]{2,1,0:T(8,128)} %param.23), kind=kLoop, calls=%fused_computation.48 | loop fusion | flops 18874368 | bytes 44046348 | tf_op jit(solution)/shard_map/convert_element_type | solution.py:91
  893.0 0.0 all-gather.2.cloned.1.call-update
  893.1 45.5 %copy.45 = f32[2048,5632]{0,1:T(8,128)} copy(f32[2048,5632]{1,0:T(8,128)} %param.16) | data formatting | bytes 92274688 | tf_op args[4]
  938.5 46.1 %multiply_add_fusion = f32[3,1024,1024]{2,1,0:T(8,128)} fusion(f32[3,1024,1024]{2,1,0:T(8,128)} %param.19, f32[3,1024,1024]{2,1,0:T(8,128)} %reduce-scatter.2.cloned.1.call-done), kind=kOutput, calls=%fused_computation.4 | convolution fusion | flops 38667288576 | bytes 37748736 | tf_op jit(solution)/shard_map/nki,nkj->nij/dot_general | solution.py:52
  984.6 46.9 %multiply_add_fusion.1 = f32[3,1024,1024]{2,1,0:T(8,128)} fusion(f32[3,1024,1024]{2,1,0:T(8,128)} %param.18, f32[3,1024,1024]{2,1,0:T(8,128)} %reduce-scatter.2.cloned.1.call-done), kind=kOutput, calls=%fused_computation.5 | convolution fusion | flops 38667288576 | bytes 37748736 | tf_op jit(solution)/shard_map/nik,njk->nij/dot_general | solution.py:51
  1031.5 88.4 %all-gather.2.cloned.1.call-done = bf16[24,1024,1024]{2,1,0:T(8,128)(2,1)} async-done(((bf16[3,1024,1024]{2,1,0:T(8,128)(2,1)}), bf16[24,1024,1024]{2,1,0:T(8,128)(2,1)}) %all-gather.2.cloned.1.call-update) | async-done | bytes 50331664 | tf_op jit(solution)/shard_map/all_gather | solution.py:91
  1119.8 33.9 %fusion.26 = (bf16[12,1024,1024]{2,1,0:T(8,128)(2,1)}, bf16[12,1024,1024]{2,1,0:T(8,128)(2,1)}) fusion(bf16[24,1024,1024]{2,1,0:T(8,128)(2,1)} %all-gather.2.cloned.1.call-done), kind=kLoop, calls=%fused_computation.49 | loop fusion | bytes 100663296 | tf_op jit(solution)/shard_map/slice | solution.py:72
  1153.7 61.6 %copy.43 = bf16[2,6,1024,1024]{2,0,3,1:T(2,128)(2,1)} copy(bf16[2,6,1024,1024]{3,2,1,0:T(8,128)(2,1)} %bitcast.52) | data formatting | bytes 50331648 | tf_op jit(solution)/shard_map/reshape | solution.py:30
  1215.4 25.2 %copy.58 = bf16[768,8,2,1024]{3,1,2,0:T(8,128)(2,1)} copy(bf16[768,8,2,1024]{3,2,1,0:T(2,128)(2,1)} %bitcast.49) | data formatting | bytes 50331648
  1240.6 38.5 %multiply_subtract_fusion.1 = f32[2048,5632]{0,1:T(8,128)} fusion(f32[2048,5632]{0,1:T(8,128)} %copy.45, bf16[2048,6144]{0,1:T(8,128)(2,1)} %bitcast.53), kind=kLoop, calls=%fused_computation.2 | loop fusion | flops 57671680 | bytes 115343360 | tf_op jit(solution)/shard_map/sub | solution.py:73
  1279.1 42.3 %copy.48 = f32[2048,5632]{1,0:T(8,128)} copy(f32[2048,5632]{0,1:T(8,128)} %multiply_subtract_fusion.1) | data formatting | bytes 92274688
  1321.3 44.7 %copy.46 = bf16[6,1024,2,1024]{3,2,1,0:T(2,128)(2,1)S(1)} copy(bf16[6,1024,2,1024]{3,1,2,0:T(8,128)(2,1)} %bitcast.51) | data formatting | bytes 50331648 | tf_op jit(solution)/shard_map/transpose | solution.py:30
  1366.1 10.9 copy.59
  1377.0 38.5 %multiply_subtract_fusion = f32[5632,2048]{1,0:T(8,128)} fusion(f32[5632,2048]{1,0:T(8,128)} %param.17, bf16[6144,2048]{1,0:T(8,128)(2,1)} %bitcast.54), kind=kLoop, calls=%fused_computation.1 | loop fusion | flops 57671680 | bytes 115343360 | tf_op jit(solution)/shard_map/sub | solution.py:74
  (8 shorter events, 0.0 us)
Async XLA Ops:
  7.2 762.1 %reduce-scatter.2.cloned.1.call-start = ((), (), s32[]{:S(2)}) async-start(), calls=%async_computation.1 | async-start | bytes 113246208 | tf_op jit(solution)/shard_map/reduce_scatter | solution.py:86
  235.7 884.2 %all-gather.2.cloned.1.call-start = ((), (), s32[]{:S(2)}) async-start(), calls=%async_computation.2 | async-start | bytes 56623104 | tf_op jit(solution)/shard_map/all_gather | solution.py:91
  769.2 93.8 %slice-start = ((s8[12582912]{0:T(1024)(128)(4,1)}), s8[4194304]{0:T(1024)(128)(4,1)S(1)}, s32[]{:S(2)}) async-start(s8[12582912]{0:T(1024)(128)(4,1)} %bitcast.56), calls=%async_computation.3 | async-start | bytes 8388608
  769.2 93.8 %slice-start.1 = ((s8[12582912]{0:T(1024)(128)(4,1)}), s8[4194304]{0:T(1024)(128)(4,1)S(1)}, s32[]{:S(2)}) async-start(s8[12582912]{0:T(1024)(128)(4,1)} %bitcast.56), calls=%async_computation.4 | async-start | bytes 8388608
  814.4 48.6 %slice-start.2 = ((s8[12582912]{0:T(1024)(128)(4,1)}), s8[4194304]{0:T(1024)(128)(4,1)S(1)}, s32[]{:S(2)}) async-start(s8[12582912]{0:T(1024)(128)(4,1)} %bitcast.56), calls=%async_computation.5 | async-start | bytes 8388608
Sparse Core Ops, SparseCore 0:
  235.8 533.3 reduce-scatter.1
  893.2 226.6 all-gather.1
where the time goes:
time: 1430 us; the launch traced here: 1420 us
  waiting for transfers between devices  622 us (43%)
  local copies, waits for them, and re-layouts  359 us (25%)
  matrix products  254 us (18%)
  other arithmetic  174 us (12%)
  between operations  14.5 us (1%)
    reduce_scatter x1, waiting for transfers between devices, per_device(): lax.psum_scatter(local_grad, 'dp', scatter_dimension=0, tiled=True) / n_dev  533 us
    unnamed x12, local copies, waits for them, and re-layouts  156 us
    all_gather x1, waiting for transfers between devices, per_device(): lax.all_gather(new_mom.astype(jnp.bfloat16), 'dp', axis=0, tiled=True)  88.4 us
    dot_general x2, matrix products, grad_blocks(): jnp.einsum('tri,tcj->rcij', x_pad, dy_pad, preferred_element_type=jnp.flo...  67 us
    concatenate x1, other arithmetic, per_device(): jnp.concatenate([grad_blocks(x_in, dy_mid, block_dim), grad_blocks(x_mid,...  66.8 us
    reshape x1, local copies, waits for them, and re-layouts, from_blocks(): dir_blocks.reshape(row_blocks, col_blocks, block_dim, block_dim)  61.6 us
    transpose x1, local copies, waits for them, and re-layouts, grad_blocks(): jnp.einsum('tri,tcj->rcij', x_pad, dy_pad, preferred_element_type=jnp.flo...  49.5 us
    dot_general x1, matrix products, direction_update(): jnp.einsum('nij,njk->nik', left_mul, root_right, precision=lax.Precision....  48.6 us
  transfers between devices with their start and end apart: 2, of which 2 were waited for; matrix products, arithmetic and copies ran while one was open for 10% of the time, Pallas kernels for 0%

commit v1 on v0

v1 whole, which is shorter than its diff:
```python
import functools

import jax
import jax.numpy as jnp
from jax import lax
from jax.experimental import pallas as pl
from jax.experimental.pallas import tpu as pltpu
from jax.sharding import PartitionSpec as P


STEP = 10
STAT_DECAY = 0.999
MOM_DECAY = 0.9
GRAFT_EPS = 1e-8
LEARN_RATE = 0.01
WEIGHT_DECAY = 1e-4
BIAS_CORR = 1.0 - STAT_DECAY ** STEP


B = 1024
HALF = B // 2
LAST = 5
SLOTS = ["p1", "p2", "p3", "p4", "p5", "p6"]
HBM = pltpu.HBM
ANY_SPEC = pl.BlockSpec(memory_space=HBM)
BF16 = jnp.bfloat16
F32 = jnp.float32
MIB = 1 << 20
MESH = pl.DeviceIdType.MESH


def place():
    d = lax.axis_index("dp")
    return d // 4, (d // 2) % 2, d % 2


def tile_plan(kind, x, core):
    if kind == 0:
        return dict(p1=("s", 1 - x), p3=("s", x), p2=("l", 3 * core), p4=("l", 3 * core + 1), p5=("l", 3 * core + 2))
    far, own = 3 * (1 - x), 3 * x
    return dict(p1=("s", 0), p3=("s", 1), p2=("l", far + 2 * core), p4=("l", own + 2 * core),
                p5=("l", jnp.where(core == 0, far + 1, own + 1)))


def split(v):
    hi = v.astype(BF16)
    return hi, (v - hi.astype(F32)).astype(BF16)


def fold(v):
    return jnp.sum(v.reshape(v.shape[0] // 8, 8, v.shape[1]), axis=0)


def own_index(order):
    y, _, core = place()
    return jnp.where((y == 1) & (core == 1), (order + 1) % 3, order)


def each(n, step, f):
    @pl.loop(0, n // step)
    def _(r):
        f(pl.multiple_of(r * step, step))


def corners(ref):
    y, _, _ = place()
    for h in range(2):
        for q in range(2):
            yield y == 0, ref.at[pl.ds(q * HALF, HALF), pl.ds(h * HALF, HALF)], h, q
            yield y == 1, ref.at[pl.ds(h * HALF, HALF), pl.ds(q * HALF, HALF)], h, q


DIR_SCRATCH = [pltpu.VMEM((B, B), F32)] * 6 + [
    pltpu.VMEM((2, B, B), BF16), pltpu.VMEM((2, B, B), BF16), pltpu.VMEM((256, B), F32), pltpu.VMEM((B, B), BF16),
    pltpu.VMEM((8, B), F32), pltpu.VMEM((8, B), F32), pltpu.SemaphoreType.DMA((2, 2)), pltpu.SemaphoreType.DMA((4,)),
    pltpu.SemaphoreType.DMA((2,))]


def dir_loads(order, states, scr):
    root_l, root_r, graft, mom = states
    lv, rrv, av, mv, sem = scr[2], scr[3], scr[4], scr[5], scr[13]
    j = own_index(order)
    return [pltpu.make_async_copy(s.at[j], d, sem.at[i])
            for i, (s, d) in enumerate(((root_r, rrv), (root_l, lv), (graft, av), (mom, mv)))]


def dir_math(order, states, scr, g_out, mom_out, d_out):
    gv, rv, lv, rrv, av, mv, gs, rs, acc, dv, hsum, psum, sem_q, _, sem_out = scr
    loads = dir_loads(order, states, scr)
    y, x, core = place()
    block = ((x * 2 + core) * 3) + own_index(order)
    col_count = jnp.where((y == 0) & (block % 6 == LAST), HALF, B)
    row_count = jnp.where((y == 1) & (block // 2 == LAST), HALF, B)
    hsum[...] = jnp.zeros_like(hsum)
    psum[...] = jnp.zeros_like(psum)
    step = 64

    def make_grad(r):
        at = pl.ds(r, step)
        g = (gv[at, :] + rv[at, :]) * 0.125
        gv[at, :] = g
        gs[0, at, :], gs[1, at, :] = split(g)

    each(B, step, make_grad)
    g_copy = pltpu.make_async_copy(gv, g_out, sem_out.at[0])
    g_copy.start()
    loads[0].wait()

    def split_right(r):
        at = pl.ds(r, step)
        rs[0, at, :], rs[1, at, :] = split(rrv[at, :])

    each(B, step, split_right)
    loads[1].wait()
    loads[2].wait()
    rows = 256
    col = lax.broadcasted_iota(jnp.int32, (8, B), 1)

    def dot3(a_hi, a_lo, b):
        return (jnp.dot(a_hi, b[0], preferred_element_type=F32) + jnp.dot(a_hi, b[1], preferred_element_type=F32)
                + jnp.dot(a_lo, b[0], preferred_element_type=F32))

    @pl.loop(0, B // rows)
    def _(m):
        at = pl.ds(pl.multiple_of(m * rows, rows), rows)
        left = dot3(*split(lv[at, :]), gs)
        acc[...] = dot3(*split(left), rs)

        def finish(r):
            here = pl.ds(r, step)
            full = pl.ds(m * rows + r, step)
            kept = jnp.where(m * rows < row_count, col_count, 0)
            p = acc[here, :].reshape(step // 8, 8, B)
            p = jnp.where((col < kept)[None], p, 0.0)
            psum[...] += jnp.sum(p * p, axis=0)
            rv[full, :] = p.reshape(step, B)
            g = gv[full, :]
            sq = STAT_DECAY * av[full, :] + (1.0 - STAT_DECAY) * g * g
            h = g / (jnp.sqrt(sq * (1.0 / BIAS_CORR)) + GRAFT_EPS)
            hsum[...] += fold(h * h)

        each(rows, step, finish)

    def total(v):
        return jnp.sum(jnp.sum(v[...], axis=0, keepdims=True), axis=1, keepdims=True)

    ratio = jnp.sqrt(total(hsum)) / jnp.sqrt(total(psum))
    loads[3].wait()

    def momentum(r):
        at = pl.ds(r, step)
        new = MOM_DECAY * mv[at, :] + rv[at, :] * ratio
        mv[at, :] = new
        dv[at, :] = new.astype(BF16)

    each(B, step, momentum)
    mom_copy = pltpu.make_async_copy(mv, mom_out, sem_out.at[1])
    mom_copy.start()
    for cond, view, h, q in corners(dv):
        @pl.when(cond)
        def _():
            pltpu.make_async_copy(view, d_out.at[h, q], sem_q.at[h, q]).start()
    for h in range(2):
        for q in range(2):
            pltpu.make_async_copy(dv.at[pl.ds(0, HALF), pl.ds(0, HALF)], d_out.at[h, q], sem_q.at[h, q]).wait()
    return g_copy, mom_copy


def dir_body(order, own, recv, *refs):
    states, (g_out, mom_out, d_out), scr, sem_r = refs[:4], refs[4:7], refs[7:-1], refs[-1]
    gv, rv, sem_q = scr[0], scr[1], scr[12]
    for ref, src, sem in ((gv, own, sem_q), (rv, recv, sem_r)):
        for cond, view, h, q in corners(ref):
            @pl.when(cond)
            def _():
                pltpu.make_async_copy(src.at[h, q], view, sem.at[h, q]).start()
    for c in dir_loads(order, states, scr):
        c.start()
    for h in range(2):
        for q in range(2):
            for ref, src, sem in ((gv, own, sem_q), (rv, recv, sem_r)):
                pltpu.make_async_copy(src.at[h, q], ref.at[pl.ds(0, HALF), pl.ds(0, HALF)], sem.at[h, q]).wait()
    for c in dir_math(order, states, scr, g_out, mom_out, d_out):
        c.wait()


def direction(order, own, recv, states):
    tile = jax.ShapeDtypeStruct((B, B), F32)
    return pl.pallas_call(
        functools.partial(dir_body, order),
        out_shape=[tile, tile, jax.ShapeDtypeStruct((2, 2, HALF, HALF), BF16)],
        in_specs=[ANY_SPEC] * 6,
        out_specs=[ANY_SPEC] * 3,
        scratch_shapes=DIR_SCRATCH + [pltpu.SemaphoreType.DMA((2, 2))],
        compiler_params=pltpu.CompilerParams(vmem_limit_bytes=56 * MIB),
        cost_estimate=pl.CostEstimate(flops=12 * B * B * B, bytes_accessed=36 * MIB, transcendentals=3 * B * B),
    )(own, recv, *states)


Y_PIECES = [(n, h, t) for n, ts in (("p1", "s"), ("p2", "sx"), ("p3", "s"), ("p4", "sx"), ("p5", "sx")) for h in (0, 1) for t in ts]
RELAYS = [("p1", 0), ("p1", 1), ("p3", 0), ("p3", 1), ("s5", 0), ("x5", 0), ("s5", 1), ("x5", 1)]
SIBLINGS = [(n, h) for n in SLOTS for h in (0, 1)]
SENT = ((("p1", "p2"), ("p1", "p2"), ("p1", "p2")),
        (("p1", "p4"), ("p3", "p2"), ("p3", "p2")),
        (("p1", "p5"), ("p1", "p5"), ("p3", "p6")))
KEPT = ((("p3", "p2"), ("p1", "p4"), ("p1", "p4")),
        (("p3", "p4"), ("p3", "p4"), ("p3", "p4")),
        (("p3", "p5"), ("p1", "p6"), ("p3", "p5")))


def front_body(x_in, dy_mid, x_mid, dy_out, root_l, root_r, graft, mom,
               ry, rc, rsib, own2, recv2, g0, g1, mo0, mo1, d0, d1, dr0, xr,
               buf, xacc, y_send, y_recv, c_send, c_recv, s_send, s_recv, x_send, x_recv, d_send, d_recv,
               op_sem, r_sem, o_sem, *scr):
    states = (root_l, root_r, graft, mom)
    gv, rv = scr[0], scr[1]
    me = lax.axis_index("dp")
    y, x, core = place()
    roles = (y == 0, (y == 1) & (core == 0), (y == 1) & (core == 1))
    arrays = {(0, "s"): x_in, (0, "l"): dy_mid, (1, "s"): dy_out, (1, "l"): x_mid}
    first = y == 0

    def peer(mask):
        return lax.bitwise_xor(me, jnp.int32(mask))

    barrier = pltpu.get_barrier_semaphore()
    for mask in (1, 2, 4, 5):
        pl.semaphore_signal(barrier, inc=1, device_id=(peer(mask),), device_id_type=MESH)
    pl.semaphore_wait(barrier, 4)

    def plan(kind, c, name):
        return tile_plan(kind, x, 1 - c)["p5"] if name == "p6" else tile_plan(kind, x, c)[name]

    def view(kind, c, name, half):
        form, tile = plan(kind, c, name)
        cols = pl.ds(pl.multiple_of(tile * B + half * HALF, HALF), HALF)
        return arrays[kind, form].at[:, cols], tile != LAST if form == "l" and half else True

    def real(kind, c, name, half):
        form, tile = plan(kind, c, name)
        return tile != LAST if form == "l" and half else True

    def when(cond, f):
        if cond is True:
            f()
        else:
            pl.when(cond)(f)

    def both(*conds):
        out = True
        for c in conds:
            out = c if out is True else out if c is True else out & c
        return out


    def y_copy(i, src):
        mask = 4 if Y_PIECES[i][2] == "s" else 5
        return pltpu.make_async_remote_copy(src_ref=src, dst_ref=ry.at[i], send_sem=y_send.at[i], recv_sem=y_recv.at[i],
                                            device_id=(peer(mask),), device_id_type=MESH)

    def y_each(i, act):
        name, half, t = Y_PIECES[i]
        for my_y in (0, 1):
            src, ok = view(1 - my_y, core if t == "s" else 1 - core, name, half)
            when(both(y == my_y, ok), lambda: act(y_copy(i, src)))

    def y_arrive(name, half, t):
        i = Y_PIECES.index((name, half, t))
        for my_y in (0, 1):
            when(both(y == my_y, real(my_y, core, name, half)), lambda: y_copy(i, ry.at[i]).wait_recv())

    def sib_copy(k, src):
        return pltpu.make_async_remote_copy(src_ref=src, dst_ref=rsib.at[k], send_sem=s_send.at[k], recv_sem=s_recv.at[k],
                                            device_id=(peer(1),), device_id_type=MESH)

    def sib_each(k, act):
        name, half = SIBLINGS[k]
        for my_y in (0, 1):
            if name == "p6" and my_y == 0:
                continue
            src, ok = view(my_y, 1 - core, name, half)
            when(both(y == my_y, ok), lambda: act(sib_copy(k, src)))

    def sib_arrive(k):
        name, half = SIBLINGS[k]
        for my_y in (0, 1):
            if name == "p6" and my_y == 0:
                continue
            when(both(y == my_y, real(my_y, core, name, half)), lambda: sib_copy(k, rsib.at[k]).wait_recv())

    def relay(name, half):
        k = RELAYS.index((name, half))
        piece = (name, half, "s") if name[0] == "p" else ("p5", half, name[0])
        return pltpu.make_async_remote_copy(src_ref=ry.at[Y_PIECES.index(piece)], dst_ref=rc.at[k], send_sem=c_send.at[k],
                                            recv_sem=c_recv.at[k], device_id=(peer(1),), device_id_type=MESH)

    def relay_if(name):
        return True if name[0] == "p" else y == 1

    def x_real(order, half, d_core, d_x):
        if not half:
            return True
        ok1 = (y == 1) | (d_core == 0) if order == 2 else True
        ok2 = (y == 0) | (d_core == 0) | (d_x == 1) if order < 2 else True
        return both(ok1, ok2)

    def x_copy(order, half):
        dst = recv2.at[half] if order == 2 else xr.at[order, half]
        return pltpu.make_async_remote_copy(src_ref=xacc.at[half], dst_ref=dst, send_sem=x_send.at[order, half],
                                            recv_sem=x_recv.at[order, half], device_id=(peer(2),), device_id_type=MESH)

    def source(s, name, half):
        if s == 1:
            return rsib.at[SIBLINGS.index((name, half))]
        if name in ("p1", "p3"):
            return ry.at[Y_PIECES.index((name, half, "s"))] if s == 2 else rc.at[RELAYS.index((name, half))]
        if name == "p6":
            return rc.at[RELAYS.index(("x5" if s == 2 else "s5", half))]
        return ry.at[Y_PIECES.index((name, half, "s" if s == 2 else "x"))]


    def operand(s, table, part, halves, wait):
        for role, (cond, (short, long)) in enumerate(zip(roles, table)):
            name, half = (short, part) if part < 2 else (long, halves[part - 2])
            kind = min(role, 1)
            src = source(s, name, half) if s else view(kind, core, name, half)[0]

            def go():
                copy = pltpu.make_async_copy(src, buf.at[s, part], op_sem.at[s, part])
                copy.wait() if wait else copy.start()

            when(both(cond, real(kind, core, name, half)), go)

    def product(table, halves, arrivals, put, live):
        parts = range(2 + len(halves))
        for s in range(4):
            for part in parts:
                if (s, part) not in arrivals:
                    operand(s, table, part, halves, False)
        for s in range(4):
            for part in parts:
                if (s, part) in arrivals:
                    arrivals[s, part]()
                    operand(s, table, part, halves, False)
            for part in parts:
                operand(s, table, part, halves, True)
            for i, h in enumerate(halves):
                def dots():
                    @pl.loop(0, 2)
                    def _(q):
                        lhs = jnp.where(first, q, 2 + i)
                        rhs = jnp.where(first, 2 + i, q)
                        part = lax.dot_general(buf[s, lhs], buf[s, rhs], (((0,), (0,)), ((), ())),
                                               preferred_element_type=F32)
                        put(h, q, part, s == 0)

                when(live(h), dots)

    def put_sent(h, q, part, fresh):
        xacc[h, q] = part if fresh else xacc[h, q] + part

    def put_kept(h, q, part, fresh):
        rows = pl.ds(pl.multiple_of(jnp.where(first, q, h) * HALF, HALF), HALF)
        cols = pl.ds(pl.multiple_of(jnp.where(first, h, q) * HALF, HALF), HALF)
        gv[rows, cols] = part if fresh else gv[rows, cols] + part

    def send(order, half, arrivals):
        ok = x_real(order, half, core, x)
        if order:
            when(x_real(order - 1, half, core, x), lambda: x_copy(order - 1, half).wait_send())
        product(SENT[order], (half,), arrivals, put_sent, lambda h: ok)
        when(ok, lambda: x_copy(order, half).start())

    def keep(order):
        pads = [jnp.logical_not(jnp.asarray(x_real(order, 1, core, 1 - x)))]

        def clear(q):
            def zero(r):
                rows = pl.ds(pl.multiple_of(jnp.where(first, q, 1) * HALF, HALF) + r, 64)
                cols = pl.ds(pl.multiple_of(jnp.where(first, 1, q) * HALF, HALF), HALF)
                gv[rows, cols] = jnp.zeros((64, HALF), F32)

            each(HALF, 64, zero)

        @pl.when(pads[0])
        def _():
            clear(0)
            clear(1)

        product(KEPT[order], (0, 1), {}, put_kept, lambda h: True if h == 0 else x_real(order, 1, core, 1 - x))

    def take(order):
        for half in (0, 1):
            ok = x_real(order, half, core, 1 - x)
            when(ok, lambda: x_copy(order, half).wait_recv())
            for cond, spot, h, q in corners(rv):
                if h == half:
                    when(both(cond, ok), lambda: pltpu.make_async_copy(xr.at[order, h, q], spot, r_sem.at[h, q]).start())
            if half and ok is not True:
                for cond, spot, h, q in corners(rv):
                    if h == half:
                        def zero(r):
                            spot[pl.ds(r, 64), :] = jnp.zeros((64, HALF), F32)

                        when(both(cond, jnp.logical_not(ok)), lambda: each(HALF, 64, zero))
        for half in (0, 1):
            ok = x_real(order, half, core, 1 - x)
            for q in (0, 1):
                corner = rv.at[pl.ds(0, HALF), pl.ds(0, HALF)]
                when(ok, lambda: pltpu.make_async_copy(xr.at[order, half, q], corner, r_sem.at[half, q]).wait())


    for i in range(len(Y_PIECES)):
        y_each(i, lambda c: c.start())
    for k in range(len(SIBLINGS)):
        sib_each(k, lambda c: c.start())
    for c in dir_loads(0, states, scr):
        c.start()
    for k in range(len(SIBLINGS)):
        sib_arrive(k)
    for h in (0, 1):
        y_arrive("p1", h, "s")
        relay("p1", h).start()
    for h in (0, 1):
        relay("p1", h).wait_recv()
    for h in (0, 1):
        send(0, h, {(2, 2): lambda: y_arrive("p2", h, "s"), (3, 2): lambda: y_arrive("p2", h, "x")})
    for h in (0, 1):
        y_arrive("p3", h, "s")
        relay("p3", h).start()
    for h in (0, 1):
        relay("p3", h).wait_recv()
    for h in (0, 1):
        send(1, h, {(2, 2): lambda: y_arrive("p4", h, "s"), (3, 2): lambda: y_arrive("p4", h, "x")})
    keep(0)
    take(0)
    copies = dir_math(0, states, scr, g0, mo0, d0)
    to_y = pltpu.make_async_remote_copy(src_ref=d0, dst_ref=dr0, send_sem=d_send.at[0], recv_sem=d_recv.at[0],
                                        device_id=(peer(4),), device_id_type=MESH)
    to_y.start()

    def last_arrivals(h):
        for t in "sx":
            y_arrive("p5", h, t)
            when(y == 1, lambda: relay(t + "5", h).start())
        for t in "sx":
            when(y == 1, lambda: relay(t + "5", h).wait_recv())

    send(2, 0, {(2, 2): lambda: last_arrivals(0), (3, 2): lambda: None})
    for c in copies:
        c.wait()
    for c in dir_loads(1, states, scr):
        c.start()
    keep(1)
    take(1)
    copies = dir_math(1, states, scr, g1, mo1, d1)
    send(2, 1, {(2, 2): lambda: last_arrivals(1), (3, 2): lambda: None})
    for c in copies:
        c.wait()
    keep(2)
    for cond, spot, h, q in corners(gv):
        when(cond, lambda: pltpu.make_async_copy(spot, own2.at[h, q], o_sem.at[h, q]).start())
    for h in (0, 1):
        for q in (0, 1):
            pltpu.make_async_copy(gv.at[pl.ds(0, HALF), pl.ds(0, HALF)], own2.at[h, q], o_sem.at[h, q]).wait()
    pad = jnp.logical_not(jnp.asarray(x_real(2, 1, core, 1 - x)))

    @pl.when(pad)
    def _():
        def zero(r):
            rv[pl.ds(r, 64), :HALF] = jnp.zeros((64, HALF), F32)

        each(HALF, 64, zero)
        fill = [pltpu.make_async_copy(rv.at[pl.ds(0, HALF), pl.ds(0, HALF)], recv2.at[1, q], o_sem.at[0, q]) for q in (0, 1)]
        for c in fill:
            c.start()
        for c in fill:
            c.wait()

    for half in (0, 1):
        when(x_real(2, half, core, x), lambda: x_copy(2, half).wait_send())
        when(x_real(2, half, core, 1 - x), lambda: x_copy(2, half).wait_recv())
    to_y.wait()
    for i in range(len(Y_PIECES)):
        y_each(i, lambda c: c.wait_send())
    for k in range(len(SIBLINGS)):
        sib_each(k, lambda c: c.wait_send())
    for name, h in RELAYS:
        when(relay_if(name), lambda: relay(name, h).wait_send())


def front(ins, states):
    def tiles(*shape, dtype=F32):
        return jax.ShapeDtypeStruct(shape, dtype)

    dma = pltpu.SemaphoreType.DMA
    quarter = (2, 2, HALF, HALF)
    outs = [tiles(len(Y_PIECES), B, HALF, dtype=BF16), tiles(len(RELAYS), B, HALF, dtype=BF16),
            tiles(len(SIBLINGS), B, HALF, dtype=BF16), tiles(*quarter), tiles(*quarter), tiles(B, B), tiles(B, B),
            tiles(B, B), tiles(B, B), tiles(*quarter, dtype=BF16), tiles(*quarter, dtype=BF16), tiles(*quarter, dtype=BF16),
            tiles(2, *quarter)]
    res = pl.pallas_call(
        front_body,
        out_shape=outs,
        in_specs=[ANY_SPEC] * 8,
        out_specs=[ANY_SPEC] * len(outs),
        scratch_shapes=[pltpu.VMEM((4, 4, B, HALF), BF16), pltpu.VMEM(quarter, F32),
                        dma((16,)), dma((16,)), dma((8,)), dma((8,)), dma((12,)), dma((12,)), dma((3, 2)), dma((3, 2)),
                        dma((1,)), dma((1,)), dma((4, 4)), dma((2, 2)), dma((2, 2))] + DIR_SCRATCH,
        compiler_params=pltpu.CompilerParams(vmem_limit_bytes=67_000_000, collective_id=0, has_side_effects=True),
        cost_estimate=pl.CostEstimate(flops=200_000_000_000, bytes_accessed=400 * MIB, transcendentals=0),
    )(*ins, *states)
    return res[3:12]


def stat_body(order, g, mom, stat_l, stat_r, graft, *refs):
    if order > 0:
        refs = refs[4:]
    l_out, r_out, sq_out, mom_out, gv, lv, rv, av, mv, gs, sem_in, sem_out = refs
    j = own_index(order)
    loads = [pltpu.make_async_copy(s, d, sem_in.at[i]) for i, (s, d) in enumerate(
        ((g, gv), (stat_l.at[j], lv), (stat_r.at[j], rv), (graft.at[j], av), (mom, mv)))]
    for c in loads:
        c.start()
    outs = [pltpu.make_async_copy(s, d.at[j], sem_out.at[i]) for i, (s, d) in enumerate(
        ((lv, l_out), (rv, r_out), (av, sq_out), (mv, mom_out)))]
    loads[0].wait()
    loads[3].wait()

    def prepare(r):
        at = pl.ds(r, 64)
        g = gv[at, :]
        gs[0, at, :], gs[1, at, :] = split(g)
        av[at, :] = STAT_DECAY * av[at, :] + (1.0 - STAT_DECAY) * g * g

    each(B, 64, prepare)
    outs[2].start()
    loads[4].wait()
    outs[3].start()
    loads[1].wait()
    loads[2].wait()
    rows = 256

    def product(lhs_of, dims):
        def dot(a, b):
            return lax.dot_general(lhs_of(a), gs[b], (dims, ((), ())), preferred_element_type=F32)

        return dot(0, 0) + dot(0, 1) + dot(1, 0)

    @pl.loop(0, B // rows)
    def _(m):
        at = pl.ds(pl.multiple_of(m * rows, rows), rows)
        left = product(lambda a: gs[a, at, :], ((1,), (1,)))
        lv[at, :] = STAT_DECAY * lv[at, :] + (1.0 - STAT_DECAY) * left
        right = product(lambda a: gs[a, :, at], ((0,), (0,)))
        rv[at, :] = STAT_DECAY * rv[at, :] + (1.0 - STAT_DECAY) * right

    outs[0].start()
    outs[1].start()
    for c in outs:
        c.wait()


def statistics(order, g, mom, stat_l, stat_r, graft, carried):
    tiles = jax.ShapeDtypeStruct((3, B, B), F32)
    args = [g, mom, stat_l, stat_r, graft] + list(carried)
    full = pltpu.VMEM((B, B), F32)
    return pl.pallas_call(
        functools.partial(stat_body, order),
        out_shape=[tiles] * 4,
        in_specs=[ANY_SPEC] * len(args),
        out_specs=[ANY_SPEC] * 4,
        input_output_aliases={5 + i: i for i in range(4)} if carried else {},
        scratch_shapes=[full] * 5 + [pltpu.VMEM((2, B, B), BF16), pltpu.SemaphoreType.DMA((5,)), pltpu.SemaphoreType.DMA((4,))],
        compiler_params=pltpu.CompilerParams(vmem_limit_bytes=48 * MIB),
        cost_estimate=pl.CostEstimate(flops=12 * B * B * B, bytes_accessed=36 * MIB, transcendentals=0),
    )(*args)


def weight_body(order, pieces, w1, w2, *refs):
    n = len(pieces)
    tiles = refs[:n]
    o1, o2, wv, dv, ov, sem_w, sem_d, sem_o = refs[-8:]
    depth = wv.shape[0]
    me = lax.axis_index("dp")

    def cases(i, q):
        mask, half = pieces[i]
        dev = lax.bitwise_xor(me, jnp.int32(mask))
        first = dev < 4
        j = jnp.where(jnp.logical_not(first) & (dev % 2 == 1), (order + 1) % 3, order)
        block = jnp.where(first, 3 * dev + j, 3 * (dev - 4) + j)
        r1, c1, r2, c2 = block // 6, block % 6, block // 2, block % 2
        ok1, ok2 = first, jnp.logical_not(first)
        if half:
            ok1, ok2 = ok1 & (c1 != LAST), ok2 & (r2 != LAST)
        yield ok1, w1, o1, r1 * B + q * HALF, c1 * B + half * HALF
        yield ok2, w2, o2, r2 * B + half * HALF, c2 * B + q * HALF

    def act(i, what):
        b = i % depth
        for q in range(2):
            for cond, w, o, row, col in cases(i, q):
                @pl.when(cond)
                def _():
                    here = (pl.ds(pl.multiple_of(row, HALF), HALF), pl.ds(pl.multiple_of(col, HALF), HALF))
                    if what in ("load", "wait"):
                        copy = pltpu.make_async_copy(w.at[here], wv.at[b, q], sem_w.at[b, q])
                    else:
                        copy = pltpu.make_async_copy(ov.at[b, q], o.at[here], sem_o.at[b, q])
                    copy.start() if what in ("load", "store") else copy.wait()
        if what in ("load", "wait"):
            src = tiles[i] if len(tiles[i].shape) == 3 else tiles[i].at[pieces[i][1]]
            copy = pltpu.make_async_copy(src, dv.at[b], sem_d.at[b])
            copy.start() if what == "load" else copy.wait()

    for i in range(min(depth - 1, n)):
        act(i, "load")
    for i in range(n):
        b = i % depth
        act(i, "wait")
        if i >= depth:
            act(i - depth, "drain")

        @pl.loop(0, HALF // 32)
        def _(r):
            at = pl.ds(pl.multiple_of(r * 32, 32), 32)
            w = wv[b, :, at, :]
            ov[b, :, at, :] = w - LEARN_RATE * (dv[b, :, at, :].astype(F32) + WEIGHT_DECAY * w)

        act(i, "store")
        if i + depth - 1 < n:
            act(i + depth - 1, "load")
    for i in range(max(0, n - depth), n):
        act(i, "drain")


def weights(order, pieces, w1, w2, tiles, carried):
    args = [w1, w2] + list(tiles) + list(carried)
    n = len(tiles)
    depth = min(5, n)
    wide = pltpu.VMEM((depth, 2, HALF, HALF), F32)
    return pl.pallas_call(
        functools.partial(weight_body, order, pieces),
        out_shape=[jax.ShapeDtypeStruct(w1.shape, F32), jax.ShapeDtypeStruct(w2.shape, F32)],
        in_specs=[ANY_SPEC] * len(args),
        out_specs=[ANY_SPEC] * 2,
        input_output_aliases={n + 2: 0, n + 3: 1} if carried else {},
        scratch_shapes=[wide, pltpu.VMEM((depth, 2, HALF, HALF), BF16), wide, pltpu.SemaphoreType.DMA((depth, 2)),
                        pltpu.SemaphoreType.DMA((depth,)), pltpu.SemaphoreType.DMA((depth, 2))],
        cost_estimate=pl.CostEstimate(flops=n * 1_500_000_000, bytes_accessed=5 * n * MIB, transcendentals=0),
    )(*args)


def solution(mesh):
    n_dev = mesh.shape["dp"]

    def hop(v, mask):
        return lax.ppermute(v, "dp", [(i, i ^ mask) for i in range(n_dev)])

    def step(x_in, dy_mid, x_mid, dy_out, w_fc1, w_fc2, stat_left, stat_right, root_left, root_right, graft_sq, momentum):
        states = (root_left, root_right, graft_sq, momentum)
        own2, recv2, g0, g1, mo0, mo1, d0, d1, dr0 = front((x_in, dy_mid, x_mid, dy_out), states)
        g2, mo2, d2 = direction(2, own2, recv2, states)
        stats, wts = (), ()
        for o, (g, mo, d) in enumerate(((g0, mo0, d0), (g1, mo1, d1), (g2, mo2, d2))):
            stats = statistics(o, g, mo, stat_left, stat_right, graft_sq, stats)
            t = {0: d, 4: dr0 if o == 0 else hop(d, 4), 2: hop(d, 2)}
            t[6, 0] = hop(t[4][0], 2)
            t[6, 1] = hop(t[2][1], 4)
            for m in (0, 4, 2):
                t[m + 1] = hop(t[m], 1)
            for h in (0, 1):
                t[7, h] = hop(t[6, h], 1)

            def apply(masks, carried):
                pieces = [(m, h) for m in masks for h in (0, 1)]
                return weights(o, pieces, w_fc1, w_fc2, [t[m, h] if m > 5 else t[m] for m, h in pieces], carried)

            if o < 2:
                wts = apply((0, 4, 2, 6, 1, 5, 3, 7), wts)
            else:
                wts = apply((0, 1, 4, 5, 2, 3), wts)
                wts = apply((6, 7), wts)
        return (*wts, *stats)

    row_spec = P("dp", None)
    rep_spec = P(None, None)
    tile_spec = P("dp", None, None)
    in_specs = (row_spec,) * 4 + (rep_spec,) * 2 + (tile_spec,) * 6
    out_specs = (rep_spec,) * 2 + (tile_spec,) * 4
    return jax.shard_map(step, mesh=mesh, in_specs=in_specs, out_specs=out_specs, check_vma=False)
```

time: 1430 us -> 777 us (0.54)
  Pallas kernels: 0 us -> 583 us
  waiting for transfers between devices: 622 us -> 152 us
  local copies, waits for them, and re-layouts: 359 us -> 8.81 us
  matrix products: 254 us -> 0 us
  other arithmetic: 174 us -> 0 us
  starting transfers between devices: 0.08 us -> 22.6 us
    pallas_call x0 -> x9, Pallas kernels: none -> 583 us  [the longest x1 405 us: front(): pl.pallas_call(front_body, out_shape=outs, in_specs=[ANY_SPEC] * 8, out_s...]
    reduce_scatter x1 -> x0, waiting for transfers between devices: 533 us -> none  [per_device(): lax.psum_scatter(local_grad, 'dp', scatter_dimension=0, tiled=True) / n_dev]
    dot_general x6 -> x0, matrix products: 254 us -> none  [the longest x2 67 us: grad_blocks(): jnp.einsum('tri,tcj->rcij', x_pad, dy_pad, preferred_element_type=jnp.flo...]
    unnamed x12 -> x18, local copies, waits for them, and re-layouts: 156 us -> 0.04 us
    ppermute x0 -> x26, waiting for transfers between devices: none -> 152 us  [hop(): return lax.ppermute(v, 'dp', [(i, i ^ mask) for i in range(n_dev)])]
    transpose x2 -> x0, local copies, waits for them, and re-layouts: 94.2 us -> none  [the longest x1 49.5 us: grad_blocks(): jnp.einsum('tri,tcj->rcij', x_pad, dy_pad, preferred_element_type=jnp.flo...]
    all_gather x1 -> x0, waiting for transfers between devices: 88.4 us -> none  [per_device(): lax.all_gather(new_mom.astype(jnp.bfloat16), 'dp', axis=0, tiled=True)]
    sub x2 -> x0, other arithmetic: 76.9 us -> none  [the longest x1 38.5 us: apply_update(): w_fc1 - LEARN_RATE * (dir_fc1.astype(jnp.float32) + WEIGHT_DECAY * w_fc1)]
  transfers between devices with their start and end apart: 2 -> 26, of which waited for: 2 -> 6; matrix products, arithmetic and copies ran while one was open for 10% -> 1% of each run, Pallas kernels for 0% -> 18%
where the time goes in v1:
time: 777 us; the launch traced here: 768 us
  Pallas kernels  583 us (75%)
  waiting for transfers between devices  152 us (20%)
  starting transfers between devices  22.6 us (3%)
  local copies, waits for them, and re-layouts  8.81 us (1%)
    pallas_call x1, Pallas kernels, front(): pl.pallas_call(front_body, out_shape=outs, in_specs=[ANY_SPEC] * 8, out_s...  405 us
    ppermute x26, waiting for transfers between devices, hop(): return lax.ppermute(v, 'dp', [(i, i ^ mask) for i in range(n_dev)])  152 us
    pallas_call x4, Pallas kernels, weights(): pl.pallas_call(functools.partial(weight_body, order, pieces), out_shape=[...  82.2 us
    pallas_call x3, Pallas kernels, statistics(): pl.pallas_call(functools.partial(stat_body, order), out_shape=[tiles] * 4...  68.2 us
    pallas_call x1, Pallas kernels, direction(): pl.pallas_call(functools.partial(dir_body, order), out_shape=[tile, tile,...  28.1 us
    ppermute x26, starting transfers between devices, hop(): return lax.ppermute(v, 'dp', [(i, i ^ mask) for i in range(n_dev)])  22.6 us
  transfers between devices with their start and end apart: 26, of which 6 were waited for; matrix products, arithmetic and copies ran while one was open for 1% of the time, Pallas kernels for 18%

profile of v1, /device:TPU:0, one launch (start us, length us, event | category | flops | bytes accessed | tf_op | source)
XLA Modules:
  0.0 768.1 jit_solution(12198279586439709994)
XLA Ops:
  0.6 404.8 %shard_map.163 = (bf16[16,1024,512]{2,1,0:T(8,128)(2,1)}, bf16[8,1024,512]{2,1,0:T(8,128)(2,1)}, bf16[12,1024,512]{2,1,0:T(8,128)(2,1)}, f32[2,2,512,512]{3,2,1,...) custom-call(bf16[1024,2048]{1,0:T(8,128)(2,1)} %x_in.1, ...), custom_call_target="tpu_custom_call" | custom-call | flops 199999995904 | bytes 419430400 | tf_op jit(solution)/shard_map/pallas_call | solution.py:502
  405.5 28.1 %shard_map.164 = (f32[1024,1024]{1,0:T(8,128)}, f32[1024,1024]{1,0:T(8,128)}, bf16[2,2,512,512]{3,2,1,0:T(8,128)(2,1)}) custom-call(f32[2,2,512,512]{3,2,1,0:T(8,128)} %get-tuple-element.38.own, f32[2,2,512,512]{3,2,1,0:T(8,128)} %get-tuple-element.39.recv, f32[3,1024,1024]{2,1,0:T(8,128)} %refs_0_.1, f32[3,1024,1024]{2,1,0:T(8,128)} %refs_1_.1, ...), custom_call_target="tpu_custom_call" | custom-call | flops 12884901888 | bytes 37748736 | tf_op jit(solution)/shard_map/pallas_call | solution.py:189
  433.6 13.4 %collective-permute-start = (bf16[2,2,512,512]{3,2,1,0:T(8,128)(2,1)}, bf16[2,2,512,512]{3,2,1,0:T(8,128)(2,1)S(1)}, u32[]{:S(2)}, u32[]{:S(2)}) collective-permute-start(bf16[2,2,512,512]{3,2,1,0:T(8,128)(2,1)} %get-tuple-element.40.refs_0_.refs_1_), channel_id=1, source_target_pairs={{0,4},{1,5},{2,6},{3,7},{4,0},{5,1},{6,2},{7,3}} | collective-permute-start | bytes 6291464 | tf_op jit(solution)/shard_map/ppermute | solution.py:659
  447.1 1.3 slice_bitcast_fusion.5
  448.4 2.0 collective-permute-start.2
  450.4 24.1 %collective-permute-done.19.refs_6_ = bf16[2,512,512]{2,1,0:T(8,128)(2,1)} collective-permute-done((bf16[2,512,512]{2,1,0:T(8,128)(2,1)S(1)}, bf16[2,512,512]{2,1,0:T(8,128)(2,1)}, u32[]{:S(2)}, u32[]{:S(2)}) %collective-permute-start.19) | collective-permute-done | bytes 1048608 | tf_op jit(solution)/shard_map/ppermute | solution.py:659
  474.5 19.2 %collective-permute-done.refs_4_.refs_5_ = bf16[2,2,512,512]{3,2,1,0:T(8,128)(2,1)S(1)} collective-permute-done((bf16[2,2,512,512]{3,2,1,0:T(8,128)(2,1)}, bf16[2,2,512,512]{3,2,1,0:T(8,128)(2,1)S(1)}, u32[]{:S(2)}, u32[]{:S(2)}) %collective-permute-start) | collective-permute-done | bytes 2097184 | tf_op jit(solution)/shard_map/ppermute | solution.py:659
  493.8 23.2 %shard_map.169 = (f32[3,1024,1024]{2,1,0:T(8,128)}, f32[3,1024,1024]{2,1,0:T(8,128)}, f32[3,1024,1024]{2,1,0:T(8,128)}, f32[3,1024,1024]{2,1,0:T(8,128)}) custom-call(f32[1024,1024]{1,0:T(8,128)S(1)} %copy-done.2, f32[1024,1024]{1,0:T(8,128)} %get-tuple-element.57.mom, f32[3,1024,1024]{2,1,0:T(8,128)} %stat_l.5, f32[3,1024,1024]{2,1,0:T(8,128)} %stat_r.5, ...), custom_call_target="tpu_custom_call" | custom-call | flops 12884901888 | bytes 37748736 | tf_op jit(solution)/shard_map/pallas_call | solution.py:568
  517.0 2.4 collective-permute-done.2.refs_8_.refs_9_
  519.3 45.0 %collective-permute-done.18.refs_4_.refs_5_ = bf16[2,2,512,512]{3,2,1,0:T(8,128)(2,1)} collective-permute-done((bf16[2,2,512,512]{3,2,1,0:T(8,128)(2,1)}, bf16[2,2,512,512]{3,2,1,0:T(8,128)(2,1)}, u32[]{:S(2)}, u32[]{:S(2)}) %collective-permute-start.18) | collective-permute-done | bytes 2097184 | tf_op jit(solution)/shard_map/ppermute | solution.py:659
  564.4 2.3 slice_bitcast_fusion
  566.7 0.5 collective-permute-start.24
  567.2 41.3 %collective-permute-done.10.refs_4_.refs_5_ = bf16[2,2,512,512]{3,2,1,0:T(8,128)(2,1)} collective-permute-done((bf16[2,2,512,512]{3,2,1,0:T(8,128)(2,1)}, bf16[2,2,512,512]{3,2,1,0:T(8,128)(2,1)}, u32[]{:S(2)}, u32[]{:S(2)}) %collective-permute-start.10) | collective-permute-done | bytes 2097184 | tf_op jit(solution)/shard_map/ppermute | solution.py:659
  608.8 22.3 %shard_map.170 = (f32[3,1024,1024]{2,1,0:T(8,128)}, f32[3,1024,1024]{2,1,0:T(8,128)}, f32[3,1024,1024]{2,1,0:T(8,128)}, f32[3,1024,1024]{2,1,0:T(8,128)}) custom-call(f32[1024,1024]{1,0:T(8,128)S(1)} %copy-done.1, f32[1024,1024]{1,0:T(8,128)} %get-tuple-element.55.mom, ...), custom_call_target="tpu_custom_call", output_to_operand_aliasing={{0}: (5, {}), {1}: (6, {}), {2}: (7, {}), {3}: (8, {})} | custom-call | flops 12884901888 | bytes 37748736 | tf_op jit(solution)/shard_map/pallas_call | solution.py:568
  631.1 1.0 slice_bitcast_fusion.4
  632.2 1.8 slice_bitcast_fusion.2
  634.0 1.3 slice_bitcast_fusion.1
  635.3 0.3 collective-permute-start.1
  635.6 1.7 collective-permute-start.11
  637.4 1.7 collective-permute-start.12
  639.1 22.7 %shard_map.171 = (f32[3,1024,1024]{2,1,0:T(8,128)}, f32[3,1024,1024]{2,1,0:T(8,128)}, f32[3,1024,1024]{2,1,0:T(8,128)}, f32[3,1024,1024]{2,1,0:T(8,128)}) custom-call(f32[1024,1024]{1,0:T(8,128)S(1)} %copy-done, f32[1024,1024]{1,0:T(8,128)} %get-tuple-element.53.mom, ...), custom_call_target="tpu_custom_call", output_to_operand_aliasing={{0}: (5, {}), {1}: (6, {}), {2}: (7, {}), {3}: (8, {})} | custom-call | flops 12884901888 | bytes 37748736 | tf_op jit(solution)/shard_map/pallas_call | solution.py:568
  661.9 1.0 slice_bitcast_fusion.3
  663.0 0.4 collective-permute-start.3
  663.3 19.8 %collective-permute-done.11.refs_6_ = bf16[2,512,512]{2,1,0:T(8,128)(2,1)} collective-permute-done((bf16[2,512,512]{2,1,0:T(8,128)(2,1)S(1)}, bf16[2,512,512]{2,1,0:T(8,128)(2,1)}, u32[]{:S(2)}, u32[]{:S(2)}) %collective-permute-start.11) | collective-permute-done | bytes 1048608 | tf_op jit(solution)/shard_map/ppermute | solution.py:659
  683.2 0.5 collective-permute-start.15
  683.7 0.5 collective-permute-start.17
  684.2 27.0 %shard_map.165 = (f32[2048,5632]{1,0:T(8,128)}, f32[5632,2048]{1,0:T(8,128)}) custom-call(f32[2048,5632]{1,0:T(8,128)} %w1.7, f32[5632,2048]{1,0:T(8,128)} %w2.7, bf16[2,2,512,512]{3,2,1,0:T(8,128)(2,1)} %get-tuple-element.42.refs_0_.refs_1_, bf16[2,2,512,512]{3,2,1,0:T(8,128)(2,1)} %get-tuple-element.42.refs_0_.refs_1_, ...), custom_call_target="tpu_custom_call" | custom-call | flops 24000000000 | bytes 83886080 | tf_op jit(solution)/shard_map/pallas_call | solution.py:643
  711.2 0.5 collective-permute-start.7
  711.8 0.5 collective-permute-start.4
  712.3 27.0 %shard_map.166 = (f32[2048,5632]{1,0:T(8,128)}, f32[5632,2048]{1,0:T(8,128)}) custom-call(f32[2048,5632]{1,0:T(8,128)} %w1.7, f32[5632,2048]{1,0:T(8,128)} %w2.7, bf16[2,2,512,512]{3,2,1,0:T(8,128)(2,1)} %get-tuple-element.41.refs_0_.refs_1_, ...), custom_call_target="tpu_custom_call", output_to_operand_aliasing={{0}: (18, {}), {1}: (19, {})} | custom-call | flops 24000000000 | bytes 83886080 | tf_op jit(solution)/shard_map/pallas_call | solution.py:643
  739.3 19.0 %shard_map.167 = (f32[2048,5632]{1,0:T(8,128)}, f32[5632,2048]{1,0:T(8,128)}) custom-call(f32[2048,5632]{1,0:T(8,128)} %w1.7, f32[5632,2048]{1,0:T(8,128)} %w2.7, bf16[2,2,512,512]{3,2,1,0:T(8,128)(2,1)} %get-tuple-element.40.refs_0_.refs_1_, ...), custom_call_target="tpu_custom_call", output_to_operand_aliasing={{0}: (14, {}), {1}: (15, {})} | custom-call | flops 17999998976 | bytes 62914560 | tf_op jit(solution)/shard_map/pallas_call | solution.py:643
  758.4 9.2 %shard_map.168 = (f32[2048,5632]{1,0:T(8,128)}, f32[5632,2048]{1,0:T(8,128)}) custom-call(f32[2048,5632]{1,0:T(8,128)} %w1.7, f32[5632,2048]{1,0:T(8,128)} %w2.7, bf16[2,512,512]{2,1,0:T(8,128)(2,1)} %copy-done.8, bf16[2,512,512]{2,1,0:T(8,128)(2,1)} %collective-permute-done.3.refs_1_, ...), custom_call_target="tpu_custom_call", output_to_operand_aliasing={{0}: (6, {}), {1}: (7, {})} | custom-call | flops 6000000000 | bytes 20971520 | tf_op jit(solution)/shard_map/pallas_call | solution.py:643
  (53 shorter events, 0.7 us)
Async XLA Ops:
  405.5 88.3 %copy-start.2 = (f32[1024,1024]{1,0:T(8,128)S(1)}, f32[1024,1024]{1,0:T(8,128)}, u32[]{:S(2)}) copy-start(f32[1024,1024]{1,0:T(8,128)} %get-tuple-element.56.g) | copy-start | bytes 12582916
  433.6 60.1 %collective-permute-start = (bf16[2,2,512,512]{3,2,1,0:T(8,128)(2,1)}, bf16[2,2,512,512]{3,2,1,0:T(8,128)(2,1)S(1)}, u32[]{:S(2)}, u32[]{:S(2)}) collective-permute-start(bf16[2,2,512,512]{3,2,1,0:T(8,128)(2,1)} %get-tuple-element.40.refs_0_.refs_1_), channel_id=1, source_target_pairs={{0,4},{1,5},{2,6},{3,7},{4,0},{5,1},{6,2},{7,3}} | collective-permute-start | bytes 6291464 | tf_op jit(solution)/shard_map/ppermute | solution.py:659
  448.3 26.2 %collective-permute-start.19 = (bf16[2,512,512]{2,1,0:T(8,128)(2,1)S(1)}, bf16[2,512,512]{2,1,0:T(8,128)(2,1)}, u32[]{:S(2)}, u32[]{:S(2)}) collective-permute-start(bf16[2,512,512]{2,1,0:T(8,128)(2,1)S(1)} %slice_bitcast_fusion.5), channel_id=1, source_target_pairs={{0,2},{1,3},{2,0},{3,1},{4,6},{5,7},{6,4},{7,5}} | collective-permute-start | bytes 3145736 | tf_op jit(solution)/shard_map/ppermute | solution.py:659
  448.4 71.0 %collective-permute-start.2 = (bf16[2,2,512,512]{3,2,1,0:T(8,128)(2,1)}, bf16[2,2,512,512]{3,2,1,0:T(8,128)(2,1)S(1)}, u32[]{:S(2)}, u32[]{:S(2)}) collective-permute-start(bf16[2,2,512,512]{3,2,1,0:T(8,128)(2,1)} %get-tuple-element.40.refs_0_.refs_1_), channel_id=1, source_target_pairs={{0,2},{1,3},{2,0},{3,1},{4,6},{5,7},{6,4},{7,5}} | collective-permute-start | bytes 6291464 | tf_op jit(solution)/shard_map/ppermute | solution.py:659
  450.4 114.0 %collective-permute-start.18 = (bf16[2,2,512,512]{3,2,1,0:T(8,128)(2,1)}, bf16[2,2,512,512]{3,2,1,0:T(8,128)(2,1)}, u32[]{:S(2)}, u32[]{:S(2)}) collective-permute-start(bf16[2,2,512,512]{3,2,1,0:T(8,128)(2,1)} %get-tuple-element.42.refs_0_.refs_1_), channel_id=1, source_target_pairs={{0,2},{1,3},{2,0},{3,1},{4,6},{5,7},{6,4},{7,5}} | collective-permute-start | bytes 6291464 | tf_op jit(solution)/shard_map/ppermute | solution.py:659
  450.4 116.2 %collective-permute-start.9 = (bf16[2,2,512,512]{3,2,1,0:T(8,128)(2,1)}, bf16[2,2,512,512]{3,2,1,0:T(8,128)(2,1)}, u32[]{:S(2)}, u32[]{:S(2)}) collective-permute-start(bf16[2,2,512,512]{3,2,1,0:T(8,128)(2,1)} %get-tuple-element.41.refs_0_.refs_1_), channel_id=1, source_target_pairs={{0,4},{1,5},{2,6},{3,7},{4,0},{5,1},{6,2},{7,3}} | collective-permute-start | bytes 6291464 | tf_op jit(solution)/shard_map/ppermute | solution.py:659
  474.5 134.0 %collective-permute-start.10 = (bf16[2,2,512,512]{3,2,1,0:T(8,128)(2,1)}, bf16[2,2,512,512]{3,2,1,0:T(8,128)(2,1)}, u32[]{:S(2)}, u32[]{:S(2)}) collective-permute-start(bf16[2,2,512,512]{3,2,1,0:T(8,128)(2,1)} %get-tuple-element.41.refs_0_.refs_1_), channel_id=1, source_target_pairs={{0,2},{1,3},{2,0},{3,1},{4,6},{5,7},{6,4},{7,5}} | collective-permute-start | bytes 6291464 | tf_op jit(solution)/shard_map/ppermute | solution.py:659
  493.7 217.5 %copy-start.3 = (bf16[2,2,512,512]{3,2,1,0:T(8,128)(2,1)}, bf16[2,2,512,512]{3,2,1,0:T(8,128)(2,1)S(1)}, u32[]{:S(2)}) copy-start(bf16[2,2,512,512]{3,2,1,0:T(8,128)(2,1)S(1)} %collective-permute-done.refs_4_.refs_5_) | copy-start | bytes 6291460
  493.7 137.4 %collective-permute-start.13 = (bf16[2,2,512,512]{3,2,1,0:T(8,128)(2,1)}, bf16[2,2,512,512]{3,2,1,0:T(8,128)(2,1)}, u32[]{:S(2)}, u32[]{:S(2)}) collective-permute-start(bf16[2,2,512,512]{3,2,1,0:T(8,128)(2,1)} %get-tuple-element.41.refs_0_.refs_1_), channel_id=1, source_target_pairs={{0,1},{1,0},{2,3},{3,2},{4,5},{5,4},{6,7},{7,6}} | collective-permute-start | bytes 6291464 | tf_op jit(solution)/shard_map/ppermute | solution.py:659
  493.8 115.0 %copy-start.1 = (f32[1024,1024]{1,0:T(8,128)S(1)}, f32[1024,1024]{1,0:T(8,128)}, u32[]{:S(2)}) copy-start(f32[1024,1024]{1,0:T(8,128)} %get-tuple-element.54.g) | copy-start | bytes 12582916
  519.3 89.4 %copy-start.4 = (bf16[2,2,512,512]{3,2,1,0:T(8,128)(2,1)}, bf16[2,2,512,512]{3,2,1,0:T(8,128)(2,1)S(1)}, u32[]{:S(2)}) copy-start(bf16[2,2,512,512]{3,2,1,0:T(8,128)(2,1)S(1)} %collective-permute-done.2.refs_8_.refs_9_) | copy-start | bytes 6291460
  519.3 116.0 %collective-permute-start.21 = (bf16[2,2,512,512]{3,2,1,0:T(8,128)(2,1)}, bf16[2,2,512,512]{3,2,1,0:T(8,128)(2,1)S(1)}, u32[]{:S(2)}, u32[]{:S(2)}) collective-permute-start(bf16[2,2,512,512]{3,2,1,0:T(8,128)(2,1)} %get-tuple-element.42.refs_0_.refs_1_), channel_id=1, source_target_pairs={{0,1},{1,0},{2,3},{3,2},{4,5},{5,4},{6,7},{7,6}} | collective-permute-start | bytes 6291464 | tf_op jit(solution)/shard_map/ppermute | solution.py:659
  564.4 71.3 %collective-permute-start.22 = (bf16[2,2,512,512]{3,2,1,0:T(8,128)(2,1)}, bf16[2,2,512,512]{3,2,1,0:T(8,128)(2,1)S(1)}, u32[]{:S(2)}, u32[]{:S(2)}) collective-permute-start(bf16[2,2,512,512]{3,2,1,0:T(8,128)(2,1)} %get-tuple-element.43.refs_2_.refs_3_), channel_id=1, source_target_pairs={{0,1},{1,0},{2,3},{3,2},{4,5},{5,4},{6,7},{7,6}} | collective-permute-start | bytes 6291464 | tf_op jit(solution)/shard_map/ppermute | solution.py:659
  566.7 70.7 %collective-permute-start.24 = (bf16[2,512,512]{2,1,0:T(8,128)(2,1)}, bf16[2,512,512]{2,1,0:T(8,128)(2,1)}, u32[]{:S(2)}, u32[]{:S(2)}) collective-permute-start(bf16[2,512,512]{2,1,0:T(8,128)(2,1)} %collective-permute-done.19.refs_6_), channel_id=1, source_target_pairs={{0,1},{1,0},{2,3},{3,2},{4,5},{5,4},{6,7},{7,6}} | collective-permute-start | bytes 3145736 | tf_op jit(solution)/shard_map/ppermute | solution.py:659
  608.5 30.6 %collective-permute-start.20 = (bf16[2,512,512]{2,1,0:T(8,128)(2,1)}, bf16[2,512,512]{2,1,0:T(8,128)(2,1)}, u32[]{:S(2)}, u32[]{:S(2)}) collective-permute-start(bf16[2,512,512]{2,1,0:T(8,128)(2,1)} %slice_bitcast_fusion), channel_id=1, source_target_pairs={{0,4},{1,5},{2,6},{3,7},{4,0},{5,1},{6,2},{7,3}} | collective-permute-start | bytes 3145736 | tf_op jit(solution)/shard_map/ppermute | solution.py:659
  631.1 52.6 %collective-permute-start.23 = (bf16[2,2,512,512]{3,2,1,0:T(8,128)(2,1)}, bf16[2,2,512,512]{3,2,1,0:T(8,128)(2,1)}, u32[]{:S(2)}, u32[]{:S(2)}) collective-permute-start(bf16[2,2,512,512]{3,2,1,0:T(8,128)(2,1)} %collective-permute-done.18.refs_4_.refs_5_), channel_id=1, source_target_pairs={{0,1},{1,0},{2,3},{3,2},{4,5},{5,4},{6,7},{7,6}} | collective-permute-start | bytes 6291464 | tf_op jit(solution)/shard_map/ppermute | solution.py:659
  635.3 26.6 %copy-start.6 = (bf16[2,2,512,512]{3,2,1,0:T(8,128)(2,1)}, bf16[2,2,512,512]{3,2,1,0:T(8,128)(2,1)S(1)}, u32[]{:S(2)}) copy-start(bf16[2,2,512,512]{3,2,1,0:T(8,128)(2,1)S(1)} %collective-permute-done.21.refs_8_.refs_9_) | copy-start | bytes 6291460
  635.3 27.6 %collective-permute-start.1 = (bf16[2,512,512]{2,1,0:T(8,128)(2,1)}, bf16[2,512,512]{2,1,0:T(8,128)(2,1)S(1)}, u32[]{:S(2)}, u32[]{:S(2)}) collective-permute-start(bf16[2,512,512]{2,1,0:T(8,128)(2,1)} %slice_bitcast_fusion.4), channel_id=1, source_target_pairs={{0,2},{1,3},{2,0},{3,1},{4,6},{5,7},{6,4},{7,5}} | collective-permute-start | bytes 3145736 | tf_op jit(solution)/shard_map/ppermute | solution.py:659
  635.6 47.5 %collective-permute-start.11 = (bf16[2,512,512]{2,1,0:T(8,128)(2,1)S(1)}, bf16[2,512,512]{2,1,0:T(8,128)(2,1)}, u32[]{:S(2)}, u32[]{:S(2)}) collective-permute-start(bf16[2,512,512]{2,1,0:T(8,128)(2,1)S(1)} %slice_bitcast_fusion.2), channel_id=1, source_target_pairs={{0,2},{1,3},{2,0},{3,1},{4,6},{5,7},{6,4},{7,5}} | collective-permute-start | bytes 3145736 | tf_op jit(solution)/shard_map/ppermute | solution.py:659
  637.4 45.8 %collective-permute-start.12 = (bf16[2,512,512]{2,1,0:T(8,128)(2,1)S(1)}, bf16[2,512,512]{2,1,0:T(8,128)(2,1)}, u32[]{:S(2)}, u32[]{:S(2)}) collective-permute-start(bf16[2,512,512]{2,1,0:T(8,128)(2,1)S(1)} %slice_bitcast_fusion.1), channel_id=1, source_target_pairs={{0,4},{1,5},{2,6},{3,7},{4,0},{5,1},{6,2},{7,3}} | collective-permute-start | bytes 3145736 | tf_op jit(solution)/shard_map/ppermute | solution.py:659
  639.1 44.6 %collective-permute-start.25 = (bf16[2,512,512]{2,1,0:T(8,128)(2,1)}, bf16[2,512,512]{2,1,0:T(8,128)(2,1)}, u32[]{:S(2)}, u32[]{:S(2)}) collective-permute-start(bf16[2,512,512]{2,1,0:T(8,128)(2,1)} %collective-permute-done.20.refs_7_), channel_id=1, source_target_pairs={{0,1},{1,0},{2,3},{3,2},{4,5},{5,4},{6,7},{7,6}} | collective-permute-start | bytes 3145736 | tf_op jit(solution)/shard_map/ppermute | solution.py:659
  663.0 48.8 %copy-start.8 = (bf16[2,512,512]{2,1,0:T(8,128)(2,1)}, bf16[2,512,512]{2,1,0:T(8,128)(2,1)S(1)}, u32[]{:S(2)}) copy-start(bf16[2,512,512]{2,1,0:T(8,128)(2,1)S(1)} %collective-permute-done.1.refs_0_) | copy-start | bytes 3145732
  663.0 48.2 %collective-permute-start.3 = (bf16[2,512,512]{2,1,0:T(8,128)(2,1)}, bf16[2,512,512]{2,1,0:T(8,128)(2,1)}, u32[]{:S(2)}, u32[]{:S(2)}) collective-permute-start(bf16[2,512,512]{2,1,0:T(8,128)(2,1)} %slice_bitcast_fusion.3), channel_id=1, source_target_pairs={{0,4},{1,5},{2,6},{3,7},{4,0},{5,1},{6,2},{7,3}} | collective-permute-start | bytes 3145736 | tf_op jit(solution)/shard_map/ppermute | solution.py:659
  683.2 28.1 %collective-permute-start.14 = (bf16[2,2,512,512]{3,2,1,0:T(8,128)(2,1)}, bf16[2,2,512,512]{3,2,1,0:T(8,128)(2,1)}, u32[]{:S(2)}, u32[]{:S(2)}) collective-permute-start(bf16[2,2,512,512]{3,2,1,0:T(8,128)(2,1)} %collective-permute-done.9.refs_2_.refs_3_), channel_id=1, source_target_pairs={{0,1},{1,0},{2,3},{3,2},{4,5},{5,4},{6,7},{7,6}} | collective-permute-start | bytes 6291464 | tf_op jit(solution)/shard_map/ppermute | solution.py:659
  683.2 28.6 %collective-permute-start.15 = (bf16[2,2,512,512]{3,2,1,0:T(8,128)(2,1)}, bf16[2,2,512,512]{3,2,1,0:T(8,128)(2,1)}, u32[]{:S(2)}, u32[]{:S(2)}) collective-permute-start(bf16[2,2,512,512]{3,2,1,0:T(8,128)(2,1)} %collective-permute-done.10.refs_4_.refs_5_), channel_id=1, source_target_pairs={{0,1},{1,0},{2,3},{3,2},{4,5},{5,4},{6,7},{7,6}} | collective-permute-start | bytes 6291464 | tf_op jit(solution)/shard_map/ppermute | solution.py:659
  683.7 28.1 %collective-permute-start.16 = (bf16[2,512,512]{2,1,0:T(8,128)(2,1)}, bf16[2,512,512]{2,1,0:T(8,128)(2,1)}, u32[]{:S(2)}, u32[]{:S(2)}) collective-permute-start(bf16[2,512,512]{2,1,0:T(8,128)(2,1)} %collective-permute-done.11.refs_6_), channel_id=1, source_target_pairs={{0,1},{1,0},{2,3},{3,2},{4,5},{5,4},{6,7},{7,6}} | collective-permute-start | bytes 3145736 | tf_op jit(solution)/shard_map/ppermute | solution.py:659
  683.7 28.5 %collective-permute-start.17 = (bf16[2,512,512]{2,1,0:T(8,128)(2,1)}, bf16[2,512,512]{2,1,0:T(8,128)(2,1)}, u32[]{:S(2)}, u32[]{:S(2)}) collective-permute-start(bf16[2,512,512]{2,1,0:T(8,128)(2,1)} %collective-permute-done.12.refs_7_), channel_id=1, source_target_pairs={{0,1},{1,0},{2,3},{3,2},{4,5},{5,4},{6,7},{7,6}} | collective-permute-start | bytes 3145736 | tf_op jit(solution)/shard_map/ppermute | solution.py:659
  711.2 28.1 %collective-permute-start.6 = (bf16[2,2,512,512]{3,2,1,0:T(8,128)(2,1)}, bf16[2,2,512,512]{3,2,1,0:T(8,128)(2,1)}, u32[]{:S(2)}, u32[]{:S(2)}) collective-permute-start(bf16[2,2,512,512]{3,2,1,0:T(8,128)(2,1)} %get-tuple-element.40.refs_0_.refs_1_), channel_id=1, source_target_pairs={{0,1},{1,0},{2,3},{3,2},{4,5},{5,4},{6,7},{7,6}} | collective-permute-start | bytes 6291464 | tf_op jit(solution)/shard_map/ppermute | solution.py:659
  711.2 28.1 %collective-permute-start.7 = (bf16[2,2,512,512]{3,2,1,0:T(8,128)(2,1)S(1)}, bf16[2,2,512,512]{3,2,1,0:T(8,128)(2,1)}, u32[]{:S(2)}, u32[]{:S(2)}) collective-permute-start(bf16[2,2,512,512]{3,2,1,0:T(8,128)(2,1)S(1)} %collective-permute-done.refs_4_.refs_5_), channel_id=1, source_target_pairs={{0,1},{1,0},{2,3},{3,2},{4,5},{5,4},{6,7},{7,6}} | collective-permute-start | bytes 6291464 | tf_op jit(solution)/shard_map/ppermute | solution.py:659
  711.7 27.6 %collective-permute-start.8 = (bf16[2,2,512,512]{3,2,1,0:T(8,128)(2,1)}, bf16[2,2,512,512]{3,2,1,0:T(8,128)(2,1)}, u32[]{:S(2)}, u32[]{:S(2)}) collective-permute-start(bf16[2,2,512,512]{3,2,1,0:T(8,128)(2,1)} %copy-done.4), channel_id=1, source_target_pairs={{0,1},{1,0},{2,3},{3,2},{4,5},{5,4},{6,7},{7,6}} | collective-permute-start | bytes 6291464 | tf_op jit(solution)/shard_map/ppermute | solution.py:659
  711.8 46.6 %collective-permute-start.4 = (bf16[2,512,512]{2,1,0:T(8,128)(2,1)S(1)}, bf16[2,512,512]{2,1,0:T(8,128)(2,1)}, u32[]{:S(2)}, u32[]{:S(2)}) collective-permute-start(bf16[2,512,512]{2,1,0:T(8,128)(2,1)S(1)} %collective-permute-done.1.refs_0_), channel_id=1, source_target_pairs={{0,1},{1,0},{2,3},{3,2},{4,5},{5,4},{6,7},{7,6}} | collective-permute-start | bytes 3145736 | tf_op jit(solution)/shard_map/ppermute | solution.py:659
  712.3 46.1 %collective-permute-start.5 = (bf16[2,512,512]{2,1,0:T(8,128)(2,1)}, bf16[2,512,512]{2,1,0:T(8,128)(2,1)}, u32[]{:S(2)}, u32[]{:S(2)}) collective-permute-start(bf16[2,512,512]{2,1,0:T(8,128)(2,1)} %collective-permute-done.3.refs_1_), channel_id=1, source_target_pairs={{0,1},{1,0},{2,3},{3,2},{4,5},{5,4},{6,7},{7,6}} | collective-permute-start | bytes 3145736 | tf_op jit(solution)/shard_map/ppermute | solution.py:659
  (3 other events, 57.1 us)
